TPU v7x, 32 devices: a whole 2x2x4 slice. The times are simulated.
32 devices in a mesh: groups: 2 (over y), batch: 8 (over z, x), heads: 2 (over core).
Axes of the slice: x: 2, y: 2, z: 4, core: 2. Of those that a mesh axis runs over, the one named last changes fastest.
Arguments:
- storage: bfloat16 [1, 4096, 4608], P(None, ('groups', 'batch', 'heads')), parts along dimension 1, may hold values from -6 to 6
- block_table: int32 [4096], P('groups'), parts along dimension 0, may hold values from 0 to 2047, as said below
- lengths: int32 [16], P(('groups', 'batch')), parts along dimension 0, may hold values from 4 to 2048
- query: bfloat16 [16, 4, 128, 576], P(('groups', 'batch'), None, 'heads'), parts along dimension 0, may hold values from -10 to 10
Outputs:
- context: bfloat16 [16, 4, 128, 512], P(('groups', 'batch'), None, 'heads'), parts along dimension 0
There are 2 independent parts, one for each index of `groups`. A program takes and returns all parts, laid end to end along the dimension named above; each array names one. Nothing has to cross between parts.
Inputs may be any that keep to these rules, and one draw needn't show every extreme that they name: `block_table`: the entries are a permutation of 0 to 2047; entry g names block g mod 256 of sequence g // 256. Storage device k of the batch+heads order, with k = 2 b + p, holds for every batch index j exactly 16 blocks of sequences j * 1 to (j + 1) - 1, all with block numbers from p * 128 to (p + 1) * 128 - 1, in no particular order.
All inputs are finite; a program needn't handle non-finite values.
Results may differ from a plain program's by a relative error of at most 0.0031.
Values may be sent and summed in bfloat16 or wider, within the bound.
A program may use at most 64 MiB of HBM per device.

v0:
```python
import math
import jax
import jax.numpy as jnp
from jax import lax
from jax.sharding import PartitionSpec as P

LATENT = 512
ROPE = 64
HEAD_NOPE = 128
SEQ_DEV = 1
MAXLEN = 2048
BLK = 8
QTOK = 4


def partial_softmax(query_rows, key_rows, first_place, limits, score_scale):
    scores = (
        jnp.einsum("src,stc->srt", query_rows, key_rows, preferred_element_type=jnp.float32)
        * score_scale
    )
    places = first_place + jnp.arange(key_rows.shape[1], dtype=jnp.int32)
    visible = places[None, None, :] <= limits[:, :, None]
    masked = jnp.where(visible, scores, -1e30)
    highest = jnp.max(masked, axis=2)
    raised = jnp.where(visible, jnp.exp(masked - highest[:, :, None]), 0.0)
    totals = jnp.sum(raised, axis=2)
    mixed = jnp.einsum(
        "srt,stc->src",
        raised.astype(jnp.bfloat16),
        key_rows[:, :, :LATENT],
        preferred_element_type=jnp.float32,
    )
    return (highest, totals, mixed)


def local(storage, block_table, lengths, query):
    batch_count = lax.axis_size("batch")
    head_groups = lax.axis_size("heads")
    my_batch = lax.axis_index("batch")
    my_half = lax.axis_index("heads")
    slot_count = storage.shape[1]
    per_peer = slot_count // batch_count
    block_count = MAXLEN // BLK
    half_blocks = block_count // head_groups
    width = LATENT + ROPE
    zero_index = jnp.zeros((), jnp.int32)
    table_grid = block_table.reshape(batch_count, head_groups, slot_count)
    own_table = lax.dynamic_slice(
        table_grid, (my_batch, my_half, zero_index), (1, 1, slot_count)
    ).reshape(slot_count)
    owner = own_table // block_count // SEQ_DEV
    owner_table = (owner[:, None] == jnp.arange(batch_count, dtype=jnp.int32)[None, :]).astype(
        jnp.int32
    )
    rank = jnp.sum(owner_table * (jnp.cumsum(owner_table, axis=0) - 1), axis=1)
    send_place = owner * per_peer + rank
    order = (
        jnp.zeros((slot_count,), jnp.int32)
        .at[send_place]
        .set(jnp.arange(slot_count, dtype=jnp.int32))
    )
    outgoing = jnp.take(storage, order, axis=1)
    received = lax.all_to_all(outgoing, "batch", split_axis=1, concat_axis=1, tiled=True)
    sender_table = lax.dynamic_slice(
        table_grid, (zero_index, my_half, zero_index), (batch_count, 1, slot_count)
    ).reshape(batch_count, slot_count)
    sequence_ids = sender_table // block_count
    arrivals = sequence_ids // SEQ_DEV == my_batch
    arrive_place = (
        jnp.arange(batch_count, dtype=jnp.int32)[:, None] * per_peer
        + jnp.cumsum(arrivals.astype(jnp.int32), axis=1)
        - 1
    )
    target = (
        (sequence_ids - my_batch * SEQ_DEV) * half_blocks
        + sender_table % block_count
        - my_half * half_blocks
    )
    target = jnp.where(arrivals, target, slot_count)
    source = (
        jnp.zeros((slot_count,), jnp.int32)
        .at[target.reshape(-1)]
        .set(arrive_place.reshape(-1), mode="drop")
    )
    serving = jnp.take(received, source, axis=1)
    half_length = half_blocks * BLK
    seq_count = query.shape[0]
    local_keys = serving[0].reshape(seq_count, half_length * width)
    score_scale = 1.0 / math.sqrt(HEAD_NOPE + ROPE)
    every_query = lax.all_gather(query, "heads", axis=2, tiled=True)
    all_heads = every_query.shape[2]
    row_count = QTOK * all_heads
    query_rows = every_query.reshape(seq_count, row_count, width)
    draft = jnp.arange(row_count, dtype=jnp.int32) // all_heads
    limits = lengths[:, None] - QTOK + draft[None, :]
    key_rows = local_keys.reshape(seq_count, half_length, width)
    highest, totals, mixed = partial_softmax(
        query_rows, key_rows, my_half * half_length, limits, score_scale
    )
    shaped = (
        highest.reshape(1, seq_count, QTOK, all_heads),
        totals.reshape(1, seq_count, QTOK, all_heads),
        mixed.reshape(1, seq_count, QTOK, all_heads, LATENT),
    )
    pieces = (
        lax.all_to_all(shaped[0], "heads", split_axis=3, concat_axis=0, tiled=True),
        lax.all_to_all(shaped[1], "heads", split_axis=3, concat_axis=0, tiled=True),
        lax.all_to_all(shaped[2], "heads", split_axis=3, concat_axis=0, tiled=True),
    )
    overall = jnp.max(pieces[0], axis=0)
    factor = jnp.exp(pieces[0] - overall[None])
    totals = jnp.sum(pieces[1] * factor, axis=0)
    mixed = jnp.sum(pieces[2] * factor[..., None], axis=0)
    context = (mixed / totals[..., None]).astype(jnp.bfloat16)
    return context


def solution(mesh):
    in_specs = (
        P(None, ("groups", "batch", "heads"), None),
        P("groups"),
        P(("groups", "batch")),
        P(("groups", "batch"), None, "heads", None),
    )
    out_specs = P(("groups", "batch"), None, "heads", None)
    return jax.shard_map(local, mesh=mesh, in_specs=in_specs, out_specs=out_specs, check_vma=False)
```

profile of v0, /device:TPU:0, one launch (start us, length us, event | category | flops | bytes accessed | tf_op | source)
XLA Modules:
  0.0 96.7 jit_solution(5310189866146171281)
XLA Ops:
  0.0 0.8 and_select_fusion.2
  1.2 0.7 fusion.14
  1.9 0.8 compare_select_fusion.2
  3.0 1.0 %scatter_custom_fusion = s32[128]{0:T(128)S(1)} fusion(s32[128]{0:T(128)S(1)} %fusion.14, s32[128]{0:T(128)S(1)} %iota.24, s32[]{:T(128)} %constant.113.clone.1), kind=kCustom, calls=%fused_computation.74 | custom fusion | bytes 516 | tf_op jit(solution)/shard_map/scatter | solution.py:60
  4.1 4.3 %scatter_custom_fusion.1 = s32[128]{0:T(128)S(1)} fusion(s32[1024]{0:T(1024)S(1)} %bitcast.119, s32[1024]{0:T(1024)S(1)} %add_bitcast_fusion, s32[]{:T(128)} %constant.113.clone.1), kind=kCustom, calls=%fused_computation.72 | custom fusion | bytes 516 | tf_op jit(solution)/shard_map/scatter | solution.py:83
  8.4 1.3 %gather_fusion = bf16[128,4608]{1,0:T(8,128)(2,1)S(1)} fusion(bf16[128,4608]{1,0:T(8,128)(2,1)S(1)} %bitcast.103, s32[1024]{0:T(1024)S(1)} %pad_clamp_fusion.1), kind=kCustom, calls=%fused_computation.clone | custom fusion | bytes 2359808 | tf_op jit(solution)/shard_map/jit(_take)/gather | solution.py:62
  9.9 1.8 %copy.20 = bf16[1,128,4608]{2,0,1:T(2,128)(2,1)S(1)} copy(bf16[1,128,4608]{2,1,0:T(8,128)(2,1)S(1)} %bitcast_select_fusion.1) | data formatting | bytes 2359296 | tf_op jit(solution)/shard_map/jit(_take)/select_n | solution.py:62
  11.7 0.5 broadcast.454
  12.2 8.8 %reduce.8 = bf16[128,4608]{1,0:T(8,128)(2,1)} reduce(bf16[128,1,4608]{2,1,0:T(2,128)(2,1)S(1)} %bitcast.105, bf16[]{:T(256)} %broadcast.454), dimensions={1}, to_apply=%bitcast.102.reduce_sub_computation | reduce | bytes 2359298
  21.0 2.7 %reshape.485 = bf16[8,2,36864]{2,1,0:T(2,128)(2,1)} reshape(bf16[128,4608]{1,0:T(8,128)(2,1)} %reduce.8) | data formatting | bytes 2359296
  23.8 7.4 %all-to-all-start = ((bf16[8,2,36864]{2,1,0:T(2,128)(2,1)}), bf16[8,2,36864]{2,1,0:T(2,128)(2,1)S(1)}, u32[]{:S(2)}, u32[]{:S(2)}) async-start(bf16[8,2,36864]{2,1,0:T(2,128)(2,1)} %reshape.485), calls=%async_computation | async-start | bytes 2359296 | tf_op jit(solution)/shard_map/all_to_all | solution.py:63
  31.9 2.6 %all_gather.3 = bf16[1,4,128,576]{3,2,1,0:T(8,128)(2,1)} all-gather(bf16[1,4,64,576]{3,2,1,0:T(8,128)(2,1)S(1)} %copy-done.3), channel_id=1, replica_groups=mesh['groups'=2,'batch'=8,'heads'=2] {'heads'}, dimensions={2}, use_global_device_ids=true | all-gather | bytes 884736 | tf_op jit(solution)/shard_map/all_gather | solution.py:90
  34.5 25.3 %all-to-all-done = bf16[8,2,36864]{2,1,0:T(2,128)(2,1)S(1)} async-done(((bf16[8,2,36864]{2,1,0:T(2,128)(2,1)}), bf16[8,2,36864]{2,1,0:T(2,128)(2,1)S(1)}, u32[]{:S(2)}, u32[]{:S(2)}) %all-to-all-start) | async-done | bytes 1179680 | tf_op jit(solution)/shard_map/all_to_all | solution.py:63
  59.8 3.6 %reshape.486 = bf16[128,1,4608]{2,1,0:T(2,128)(2,1)} reshape(bf16[8,2,36864]{2,1,0:T(2,128)(2,1)S(1)} %all-to-all-done) | data formatting | bytes 2359296
  63.3 1.8 %copy.19 = bf16[1,128,4608]{2,1,0:T(8,128)(2,1)S(1)} copy(bf16[1,128,4608]{2,0,1:T(2,128)(2,1)} %bitcast.106) | data formatting | bytes 2359296
  65.2 1.3 %gather_fusion.1 = bf16[128,4608]{1,0:T(8,128)(2,1)S(1)} fusion(bf16[128,4608]{1,0:T(8,128)(2,1)S(1)} %bitcast.104, s32[1024]{0:T(1024)S(1)} %pad_clamp_fusion), kind=kCustom, calls=%fused_computation.1.clone | custom fusion | bytes 2359808 | tf_op jit(solution)/shard_map/jit(_take)/gather | solution.py:85
  66.6 1.9 %reshape.428 = bf16[1024,576]{1,0:T(8,128)(2,1)} reshape(bf16[1,128,4608]{2,1,0:T(8,128)(2,1)S(1)} %bitcast_select_fusion) | data formatting | bytes 2359296 | tf_op jit(solution)/shard_map/reshape.5
  68.5 1.9 %reshape_reshape_squeeze.3 = bf16[1,1024,576]{2,1,0:T(8,128)(2,1)} reshape(bf16[1,128,4608]{2,1,0:T(8,128)(2,1)S(1)} %bitcast_select_fusion) | data formatting | bytes 2359296 | tf_op jit(solution)/shard_map/reshape;reshape;squeeze | solution.py:96
  70.4 2.5 %fusion = (f32[512]{0:T(512)S(1)}, f32[1024,512]{0,1:T(8,128)S(1)}) fusion(s32[1024]{0:T(1024)S(1)} %iota_add_fusion, s32[512]{0:T(512)S(1)} %fusion.10, bf16[1024,576]{1,0:T(8,128)(2,1)} %reshape.428, bf16[512,576]{1,0:T(8,128)(2,1)S(1)} %bitcast.112), kind=kOutput, calls=%fused_computation.6 | convolution fusion | flops 606076416 | bytes 3874816 | tf_op jit(solution)/shard_map/src,stc->srt/dot_general | solution.py:18
  72.9 1.6 %fusion.1 = (f32[512]{0:T(512)S(1)}, bf16[512,1024]{1,0:T(8,128)(2,1)}) fusion(f32[1024,512]{0,1:T(8,128)S(1)} %get-tuple-element.11, f32[512]{0:T(512)S(1)} %get-tuple-element.10, s32[1024]{0:T(1024)S(1)} %iota_add_fusion, s32[512]{0:T(512)S(1)} %fusion.10), kind=kLoop, calls=%fused_computation.8 | loop fusion | flops 3669504 | bytes 3155968 | tf_op jit(solution)/shard_map/reduce_sum | solution.py:26
  74.6 0.5 broadcast.455
  75.1 0.8 reduce.11
  76.1 3.7 %all_to_all.62 = f32[2,1,256]{2,1,0:T(1,128)S(1)} all-to-all(f32[2,1,256]{2,1,0:T(1,128)S(1)} %reshape.489), channel_id=1, replica_groups=mesh['groups'=2,'batch'=8,'heads'=2] {'heads'}, dimensions={0} | all-to-all | bytes 4096 | tf_op jit(solution)/shard_map/all_to_all | solution.py:107
  79.8 0.7 reduce.12
  80.7 0.8 reduce.9
  81.6 3.7 %all_to_all.63 = f32[2,1,256]{2,1,0:T(1,128)S(1)} all-to-all(f32[2,1,256]{2,1,0:T(1,128)S(1)} %reshape.487), channel_id=1, replica_groups=mesh['groups'=2,'batch'=8,'heads'=2] {'heads'}, dimensions={0} | all-to-all | bytes 4096 | tf_op jit(solution)/shard_map/all_to_all | solution.py:106
  85.3 0.7 reduce.10
  86.1 1.9 %convolution_bitcast_fusion = f32[1,1,4,128,512]{4,3,2,1,0:T(8,128)S(1)} fusion(bf16[4,128,1024]{2,1,0:T(8,128)(2,1)} %bitcast.111, bf16[1,1024,576]{2,1,0:T(8,128)(2,1)S(1)} %copy-done.1), kind=kOutput, calls=%fused_computation.7 | convolution fusion | flops 536870912 | bytes 3145728 | tf_op jit(solution)/shard_map/srt,stc->src/dot_general | solution.py:27
  88.1 1.7 %copy.12 = f32[1,1,4,128,512]{4,2,1,0,3:T(4,128)} copy(f32[1,1,4,128,512]{4,3,2,1,0:T(8,128)S(1)} %convolution_bitcast_fusion) | data formatting | bytes 2097152 | tf_op jit(solution)/shard_map/srt,stc->src/dot_general | solution.py:27
  89.7 3.6 %all-to-all-start.1 = ((f32[1,1,4,128,512]{4,2,1,0,3:T(4,128)}), f32[1,1,4,128,512]{4,2,1,0,3:T(4,128)S(1)}, u32[]{:S(2)}, u32[]{:S(2)}) async-start(f32[1,1,4,128,512]{4,2,1,0,3:T(4,128)} %copy.12), calls=%async_computation.1 | async-start | bytes 2097152 | tf_op jit(solution)/shard_map/all_to_all | solution.py:108
  93.4 2.0 %all-to-all-done.1 = f32[1,1,4,128,512]{4,2,1,0,3:T(4,128)S(1)} async-done(((f32[1,1,4,128,512]{4,2,1,0,3:T(4,128)}), f32[1,1,4,128,512]{4,2,1,0,3:T(4,128)S(1)}, u32[]{:S(2)}, u32[]{:S(2)}) %all-to-all-start.1) | async-done | bytes 1048608 | tf_op jit(solution)/shard_map/all_to_all | solution.py:108
  96.0 0.7 copy.15
  (36 shorter events, 2.5 us)
Async XLA Ops:
  0.0 8.4 %copy-start = (bf16[1,128,4608]{2,1,0:T(8,128)(2,1)S(1)}, bf16[1,128,4608]{2,1,0:T(8,128)(2,1)}, u32[]{:S(2)}) copy-start(bf16[1,128,4608]{2,1,0:T(8,128)(2,1)} %param.6) | copy-start | bytes 3538948
  23.8 8.1 %copy-start.3 = (bf16[1,4,64,576]{3,2,1,0:T(8,128)(2,1)S(1)}, bf16[1,4,64,576]{3,2,1,0:T(8,128)(2,1)}, u32[]{:S(2)}) copy-start(bf16[1,4,64,576]{3,2,1,0:T(8,128)(2,1)} %param.9) | copy-start | bytes 884740
  23.8 36.0 %all-to-all-start = ((bf16[8,2,36864]{2,1,0:T(2,128)(2,1)}), bf16[8,2,36864]{2,1,0:T(2,128)(2,1)S(1)}, u32[]{:S(2)}, u32[]{:S(2)}) async-start(bf16[8,2,36864]{2,1,0:T(2,128)(2,1)} %reshape.485), calls=%async_computation | async-start | bytes 2359296 | tf_op jit(solution)/shard_map/all_to_all | solution.py:63
  68.5 1.9 %copy-start.2 = (bf16[1,4,128,576]{3,2,1,0:T(8,128)(2,1)S(1)}, bf16[1,4,128,576]{3,2,1,0:T(8,128)(2,1)}, u32[]{:S(2)}) copy-start(bf16[1,4,128,576]{3,2,1,0:T(8,128)(2,1)} %all_gather.3) | copy-start | bytes 1769476
  72.9 13.3 %copy-start.1 = (bf16[1,1024,576]{2,1,0:T(8,128)(2,1)S(1)}, bf16[1,1024,576]{2,1,0:T(8,128)(2,1)}, u32[]{:S(2)}) copy-start(bf16[1,1024,576]{2,1,0:T(8,128)(2,1)} %reshape_reshape_squeeze.3) | copy-start | bytes 3538948
  89.7 5.7 %all-to-all-start.1 = ((f32[1,1,4,128,512]{4,2,1,0,3:T(4,128)}), f32[1,1,4,128,512]{4,2,1,0,3:T(4,128)S(1)}, u32[]{:S(2)}, u32[]{:S(2)}) async-start(f32[1,1,4,128,512]{4,2,1,0,3:T(4,128)} %copy.12), calls=%async_computation.1 | async-start | bytes 2097152 | tf_op jit(solution)/shard_map/all_to_all | solution.py:108
where the time goes:
time: 97.3 us; the launch traced here: 96.7 us
  waiting for transfers between devices  27.3 us (28%)
  local copies, waits for them, and re-layouts  25.7 us (26%)
  other arithmetic  17.4 us (18%)
  starting transfers between devices  11 us (11%)
  blocking collectives  9.98 us (10%)
  matrix products  4.39 us (5%)
    all_to_all x1, waiting for transfers between devices, local(): lax.all_to_all(outgoing, 'batch', split_axis=1, concat_axis=1, tiled=True)  25.3 us
    unnamed x3, other arithmetic  10.5 us
    unnamed x17, local copies, waits for them, and re-layouts  9.66 us
    all_to_all x1, starting transfers between devices, local(): lax.all_to_all(outgoing, 'batch', split_axis=1, concat_axis=1, tiled=True)  7.41 us
    scatter x1, local copies, waits for them, and re-layouts, local(): source = jnp.zeros((slot_count,), jnp.int32).at[target.reshape(-1)].set(a...  4.3 us
    all_to_all x1, blocking collectives, local(): lax.all_to_all(shaped[0], 'heads', split_axis=3, concat_axis=0, tiled=True)  3.7 us
    all_to_all x1, blocking collectives, local(): lax.all_to_all(shaped[1], 'heads', split_axis=3, concat_axis=0, tiled=True)  3.7 us
    all_to_all x1, starting transfers between devices, local(): lax.all_to_all(shaped[2], 'heads', split_axis=3, concat_axis=0, tiled=True)  3.58 us
  transfers between devices with their start and end apart: 2, of which 2 were waited for; matrix products, arithmetic and copies ran while one was open for 0% of the time, Pallas kernels for 0%

commit v1 on v0

--- a/solution.py
+++ b/solution.py
@@ -60,7 +60,10 @@
         .set(jnp.arange(slot_count, dtype=jnp.int32))
     )
     outgoing = jnp.take(storage, order, axis=1)
-    received = lax.all_to_all(outgoing, "batch", split_axis=1, concat_axis=1, tiled=True)
+    received = jnp.concatenate(
+        lax.all_to_all(jnp.stack(jnp.split(outgoing, lax.axis_size("batch"), 1)), "batch", 0, 0),
+        axis=1,
+    )
     sender_table = lax.dynamic_slice(
         table_grid, (zero_index, my_half, zero_index), (batch_count, 1, slot_count)
     ).reshape(batch_count, slot_count)

time: 97.3 us -> 77.8 us (0.80)
  other arithmetic: 17.4 us -> 7.9 us
  local copies, waits for them, and re-layouts: 25.7 us -> 20.6 us
  waiting for transfers between devices: 27.3 us -> 22.7 us
    unnamed x3 -> x2, other arithmetic: 10.5 us -> 1.61 us
    all_to_all x1, waiting for transfers between devices: 25.3 us -> 20.7 us  [local(): lax.all_to_all(jnp.stack(jnp.split(outgoing, lax.axis_size('batch'), 1)),...]
    unnamed x17 -> x22, local copies, waits for them, and re-layouts: 9.66 us -> 5.69 us
    select_n x1 -> x0, local copies, waits for them, and re-layouts: 1.82 us -> none  [local(): outgoing = jnp.take(storage, order, axis=1)]
    another operation x1 -> x2, local copies, waits for them, and re-layouts: 1.9 us -> 2.56 us
  transfers between devices with their start and end apart: 2 -> 2, of which waited for: 2 -> 2; matrix products, arithmetic and copies ran while one was open for 0% -> 6% of each run, Pallas kernels for 0% -> 0%
where the time goes in v1:
time: 77.8 us; the launch traced here: 77.3 us
  waiting for transfers between devices  22.7 us (29%)
  local copies, waits for them, and re-layouts  20.6 us (26%)
  starting transfers between devices  11 us (14%)
  blocking collectives  9.8 us (13%)
  other arithmetic  7.9 us (10%)
  matrix products  4.38 us (6%)
  between operations  0.92 us (1%)
    all_to_all x1, waiting for transfers between devices, local(): lax.all_to_all(jnp.stack(jnp.split(outgoing, lax.axis_size('batch'), 1)),...  20.7 us
    all_to_all x1, starting transfers between devices, local(): lax.all_to_all(jnp.stack(jnp.split(outgoing, lax.axis_size('batch'), 1)),...  7.41 us
    unnamed x22, local copies, waits for them, and re-layouts  5.69 us
    scatter x1, local copies, waits for them, and re-layouts, local(): source = jnp.zeros((slot_count,), jnp.int32).at[target.reshape(-1)].set(a...  4.3 us
    all_to_all x1, blocking collectives, local(): lax.all_to_all(shaped[1], 'heads', split_axis=3, concat_axis=0, tiled=True)  3.7 us
    all_to_all x1, blocking collectives, local(): lax.all_to_all(shaped[0], 'heads', split_axis=3, concat_axis=0, tiled=True)  3.7 us
    all_to_all x1, starting transfers between devices, local(): lax.all_to_all(shaped[2], 'heads', split_axis=3, concat_axis=0, tiled=True)  3.58 us
    dot_general x1, matrix products, partial_softmax(): jnp.einsum('src,stc->srt', query_rows, key_rows, preferred_element_type=j...  2.45 us
  transfers between devices with their start and end apart: 2, of which 2 were waited for; matrix products, arithmetic and copies ran while one was open for 6% of the time, Pallas kernels for 0%

profile of v1, /device:TPU:0, one launch (start us, length us, event | category | flops | bytes accessed | tf_op | source)
XLA Modules:
  0.0 77.3 jit_solution(16678191850732633052)
XLA Ops:
  0.0 0.8 %and_select_fusion.2 = s32[128]{0:T(128)S(1)} fusion(s32[8,2,128]{2,1,0:T(2,128)} %bitcast.146, s32[]{:T(128)S(6)} %select_n.126, s32[]{:T(128)S(6)} %select_n.127), kind=kLoop, calls=%fused_computation.72 | loop fusion | flops 1920 | bytes 1032 | tf_op jit(solution)/shard_map/jit(floor_divide)/jit(_where)/select_n | solution.py:51
  1.2 0.7 fusion.22
  1.9 1.0 %scatter_custom_fusion = s32[128]{0:T(128)S(1)} fusion(s32[128]{0:T(128)S(1)} %fusion.22, s32[128]{0:T(128)S(1)} %iota.24, s32[]{:T(128)} %constant.113.clone.1), kind=kCustom, calls=%fused_computation.89 | custom fusion | bytes 516 | tf_op jit(solution)/shard_map/scatter | solution.py:60
  3.0 1.3 %gather_fusion = bf16[128,4608]{1,0:T(8,128)(2,1)S(1)} fusion(bf16[128,4608]{1,0:T(8,128)(2,1)S(1)} %bitcast.131, s32[1024]{0:T(1024)S(1)} %pad_clamp_fusion.1), kind=kCustom, calls=%fused_computation.clone | custom fusion | bytes 2359808 | tf_op jit(solution)/shard_map/jit(_take)/gather | solution.py:62
  4.4 0.7 fusion.11
  5.1 0.7 fusion.10
  5.7 0.7 fusion.9
  6.4 0.7 fusion.8
  7.1 0.7 fusion.7
  7.8 0.7 fusion.6
  8.4 0.7 fusion.5
  9.1 0.7 fusion.4
  9.8 7.4 %all-to-all-start = ((bf16[8,1,16,4608]{3,2,1,0:T(8,128)(2,1)}), bf16[8,1,16,4608]{3,2,1,0:T(8,128)(2,1)S(1)}, u32[]{:S(2)}, u32[]{:S(2)}) async-start(bf16[8,1,16,4608]{3,2,1,0:T(8,128)(2,1)} %fusion.4), calls=%async_computation | async-start | bytes 2359296 | tf_op jit(solution)/shard_map/all_to_all | solution.py:64
  18.3 4.3 %scatter_custom_fusion.1 = s32[128]{0:T(128)S(1)} fusion(s32[1024]{0:T(1024)S(1)} %bitcast.145, s32[1024]{0:T(1024)S(1)} %add_bitcast_fusion, s32[]{:T(128)} %constant.113.clone.1), kind=kCustom, calls=%fused_computation.87 | custom fusion | bytes 516 | tf_op jit(solution)/shard_map/scatter | solution.py:86
  22.6 2.4 %all_gather.3 = bf16[1,4,128,576]{3,2,1,0:T(8,128)(2,1)} all-gather(bf16[1,4,64,576]{3,2,1,0:T(8,128)(2,1)S(1)} %copy-done.3), channel_id=1, replica_groups=mesh['groups'=2,'batch'=8,'heads'=2] {'heads'}, dimensions={2}, use_global_device_ids=true | all-gather | bytes 884736 | tf_op jit(solution)/shard_map/all_gather | solution.py:93
  25.1 20.7 %all-to-all-done = bf16[8,1,16,4608]{3,2,1,0:T(8,128)(2,1)S(1)} async-done(((bf16[8,1,16,4608]{3,2,1,0:T(8,128)(2,1)}), bf16[8,1,16,4608]{3,2,1,0:T(8,128)(2,1)S(1)}, u32[]{:S(2)}, u32[]{:S(2)}) %all-to-all-start) | async-done | bytes 1179680 | tf_op jit(solution)/shard_map/all_to_all | solution.py:64
  45.7 1.3 %gather_fusion.1 = bf16[128,4608]{1,0:T(8,128)(2,1)S(1)} fusion(bf16[128,4608]{1,0:T(8,128)(2,1)S(1)} %bitcast.132, s32[1024]{0:T(1024)S(1)} %pad_clamp_fusion), kind=kCustom, calls=%fused_computation.1.clone | custom fusion | bytes 2359808 | tf_op jit(solution)/shard_map/jit(_take)/gather | solution.py:88
  47.2 1.9 %reshape.432 = bf16[1024,576]{1,0:T(8,128)(2,1)} reshape(bf16[1,128,4608]{2,1,0:T(8,128)(2,1)S(1)} %bitcast_select_fusion) | data formatting | bytes 2359296 | tf_op jit(solution)/shard_map/reshape.5
  49.1 1.9 %reshape_reshape_squeeze.3 = bf16[1,1024,576]{2,1,0:T(8,128)(2,1)} reshape(bf16[1,128,4608]{2,1,0:T(8,128)(2,1)S(1)} %bitcast_select_fusion) | data formatting | bytes 2359296 | tf_op jit(solution)/shard_map/reshape;reshape;squeeze | solution.py:99
  51.0 2.5 %fusion = (f32[512]{0:T(512)S(1)}, f32[1024,512]{0,1:T(8,128)S(1)}) fusion(s32[1024]{0:T(1024)S(1)} %iota_add_fusion, s32[512]{0:T(512)S(1)} %fusion.18, bf16[1024,576]{1,0:T(8,128)(2,1)} %reshape.432, bf16[512,576]{1,0:T(8,128)(2,1)S(1)} %bitcast.138), kind=kOutput, calls=%fused_computation.6 | convolution fusion | flops 606076416 | bytes 3874816 | tf_op jit(solution)/shard_map/src,stc->srt/dot_general | solution.py:18
  53.4 1.6 %fusion.1 = (f32[512]{0:T(512)S(1)}, bf16[512,1024]{1,0:T(8,128)(2,1)}) fusion(f32[1024,512]{0,1:T(8,128)S(1)} %get-tuple-element.11, f32[512]{0:T(512)S(1)} %get-tuple-element.10, s32[1024]{0:T(1024)S(1)} %iota_add_fusion, s32[512]{0:T(512)S(1)} %fusion.18), kind=kLoop, calls=%fused_computation.8 | loop fusion | flops 3669504 | bytes 3155968 | tf_op jit(solution)/shard_map/reduce_sum | solution.py:26
  55.7 0.8 %reduce.10 = f32[128,4]{1,0:T(8,128)S(1)} reduce(f32[128,1,1,4]{3,2,1,0:T(1,128)S(1)} %bitcast.140, f32[]{:T(128)} %broadcast.454), dimensions={1,2}, to_apply=%bitcast.126.reduce_sub_computation | reduce | bytes 4100
  56.6 3.7 %all_to_all.62 = f32[2,1,256]{2,1,0:T(1,128)S(1)} all-to-all(f32[2,1,256]{2,1,0:T(1,128)S(1)} %reshape.491), channel_id=1, replica_groups=mesh['groups'=2,'batch'=8,'heads'=2] {'heads'}, dimensions={0} | all-to-all | bytes 4096 | tf_op jit(solution)/shard_map/all_to_all | solution.py:110
  60.3 0.7 reduce.11
  61.3 0.8 %reduce.8 = f32[128,4]{1,0:T(8,128)S(1)} reduce(f32[128,1,1,4]{3,2,1,0:T(1,128)S(1)} %bitcast.141, f32[]{:T(128)} %broadcast.454), dimensions={1,2}, to_apply=%bitcast.124.reduce_sub_computation | reduce | bytes 4100
  62.2 3.7 %all_to_all.63 = f32[2,1,256]{2,1,0:T(1,128)S(1)} all-to-all(f32[2,1,256]{2,1,0:T(1,128)S(1)} %reshape.489), channel_id=1, replica_groups=mesh['groups'=2,'batch'=8,'heads'=2] {'heads'}, dimensions={0} | all-to-all | bytes 4096 | tf_op jit(solution)/shard_map/all_to_all | solution.py:109
  65.9 0.7 reduce.9
  66.7 1.9 %convolution_bitcast_fusion = f32[1,1,4,128,512]{4,3,2,1,0:T(8,128)S(1)} fusion(bf16[4,128,1024]{2,1,0:T(8,128)(2,1)} %bitcast.137, bf16[1,1024,576]{2,1,0:T(8,128)(2,1)S(1)} %copy-done.1), kind=kOutput, calls=%fused_computation.7 | convolution fusion | flops 536870912 | bytes 3145728 | tf_op jit(solution)/shard_map/srt,stc->src/dot_general | solution.py:27
  68.6 1.7 %copy.9 = f32[1,1,4,128,512]{4,2,1,0,3:T(4,128)} copy(f32[1,1,4,128,512]{4,3,2,1,0:T(8,128)S(1)} %convolution_bitcast_fusion) | data formatting | bytes 2097152 | tf_op jit(solution)/shard_map/srt,stc->src/dot_general | solution.py:27
  70.3 3.6 %all-to-all-start.1 = ((f32[1,1,4,128,512]{4,2,1,0,3:T(4,128)}), f32[1,1,4,128,512]{4,2,1,0,3:T(4,128)S(1)}, u32[]{:S(2)}, u32[]{:S(2)}) async-start(f32[1,1,4,128,512]{4,2,1,0,3:T(4,128)} %copy.9), calls=%async_computation.1 | async-start | bytes 2097152 | tf_op jit(solution)/shard_map/all_to_all | solution.py:111
  74.0 2.0 %all-to-all-done.1 = f32[1,1,4,128,512]{4,2,1,0,3:T(4,128)S(1)} async-done(((f32[1,1,4,128,512]{4,2,1,0,3:T(4,128)}), f32[1,1,4,128,512]{4,2,1,0,3:T(4,128)S(1)}, u32[]{:S(2)}, u32[]{:S(2)}) %all-to-all-start.1) | async-done | bytes 1048608 | tf_op jit(solution)/shard_map/all_to_all | solution.py:111
  76.5 0.7 copy.12
  (41 shorter events, 3.1 us)
Async XLA Ops:
  0.0 3.0 %copy-start = (bf16[1,128,4608]{2,1,0:T(8,128)(2,1)S(1)}, bf16[1,128,4608]{2,1,0:T(8,128)(2,1)}, u32[]{:S(2)}) copy-start(bf16[1,128,4608]{2,1,0:T(8,128)(2,1)} %param.6) | copy-start | bytes 3538948
  9.7 7.4 %copy-start.4 = (s32[2048]{0:T(1024)S(1)}, s32[2048]{0:T(1024)}, u32[]{:S(2)}) copy-start(s32[2048]{0:T(1024)} %param.7) | copy-start | bytes 24580
  9.7 12.9 %copy-start.3 = (bf16[1,4,64,576]{3,2,1,0:T(8,128)(2,1)S(1)}, bf16[1,4,64,576]{3,2,1,0:T(8,128)(2,1)}, u32[]{:S(2)}) copy-start(bf16[1,4,64,576]{3,2,1,0:T(8,128)(2,1)} %param.9) | copy-start | bytes 884740
  9.8 36.0 %all-to-all-start = ((bf16[8,1,16,4608]{3,2,1,0:T(8,128)(2,1)}), bf16[8,1,16,4608]{3,2,1,0:T(8,128)(2,1)S(1)}, u32[]{:S(2)}, u32[]{:S(2)}) async-start(bf16[8,1,16,4608]{3,2,1,0:T(8,128)(2,1)} %fusion.4), calls=%async_computation | async-start | bytes 2359296 | tf_op jit(solution)/shard_map/all_to_all | solution.py:64
  49.1 1.9 %copy-start.2 = (bf16[1,4,128,576]{3,2,1,0:T(8,128)(2,1)S(1)}, bf16[1,4,128,576]{3,2,1,0:T(8,128)(2,1)}, u32[]{:S(2)}) copy-start(bf16[1,4,128,576]{3,2,1,0:T(8,128)(2,1)} %all_gather.3) | copy-start | bytes 1769476
  53.4 13.3 %copy-start.1 = (bf16[1,1024,576]{2,1,0:T(8,128)(2,1)S(1)}, bf16[1,1024,576]{2,1,0:T(8,128)(2,1)}, u32[]{:S(2)}) copy-start(bf16[1,1024,576]{2,1,0:T(8,128)(2,1)} %reshape_reshape_squeeze.3) | copy-start | bytes 3538948
  70.3 5.7 %all-to-all-start.1 = ((f32[1,1,4,128,512]{4,2,1,0,3:T(4,128)}), f32[1,1,4,128,512]{4,2,1,0,3:T(4,128)S(1)}, u32[]{:S(2)}, u32[]{:S(2)}) async-start(f32[1,1,4,128,512]{4,2,1,0,3:T(4,128)} %copy.9), calls=%async_computation.1 | async-start | bytes 2097152 | tf_op jit(solution)/shard_map/all_to_all | solution.py:111
